TPU v7x, 32 devices: a whole 2x2x4 slice. The times are simulated.
32 devices in a mesh: seq: 8 (over y, x, core), head: 4 (over z).
Axes of the slice: x: 2, y: 2, z: 4, core: 2. Of those that a mesh axis runs over, the one named last changes fastest.
Arguments:
- query_raw: float32 [2048, 16, 128], P('seq', 'head'), may hold values from -150 to 150
- key_raw: float32 [2048, 16, 128], P('seq', 'head'), may hold values from -150 to 150
- value_raw: float32 [2048, 16, 128], P('seq', 'head'), may hold values from -6 to 6
- query_gain: float32 [16, 128], P('head'), may hold values from 0.25 to 1.75
- key_gain: float32 [16, 128], P('head'), may hold values from 0.25 to 1.75
- cotangent: float32 [2048, 16, 128], P('seq', 'head'), may hold values from -6 to 6
Outputs:
- attended: float32 [2048, 16, 128], P('seq', 'head')
- grad_query: float32 [2048, 16, 128], P('seq', 'head')
- grad_key: float32 [2048, 16, 128], P('seq', 'head')
- grad_value: float32 [2048, 16, 128], P('seq', 'head')
All inputs are finite; a program needn't handle non-finite values.
Results may differ from a plain program's by a relative error of at most 0.00023.
Values sent between devices are 32-bit elements; how exact they have to be, the bound alone decides.
No kernel may reach another device: no remote copies, remote signals or barrier semaphores. Data moves between devices by JAX's collectives and lax.ppermute only.
A program may use at most 64 MiB of HBM per device.

v0:
```python
import jax
import jax.numpy as jnp
from jax import lax
from jax.sharding import PartitionSpec as P

epsilon = 1e-06
highest = lax.Precision.HIGHEST


def carried_in(part, axis, combine, identity, reverse):
    count = lax.axis_size(axis)
    place = lax.axis_index(axis)
    ahead = count - 1 - place if reverse else place
    gathered = lax.all_gather(part, axis)
    state = jnp.zeros_like(part) + jnp.asarray(identity, part.dtype)

    def one(hop, state):
        source = count - 1 - hop if reverse else hop
        return combine(state, lax.dynamic_index_in_dim(gathered, source, 0, False))

    return lax.fori_loop(0, ahead, one, state)


def product(form, left, right):
    return jnp.einsum(form, left, right, precision=highest, preferred_element_type=jnp.float32)


def add_states(earlier, later):
    return earlier + later


def local(query_raw, key_raw, value_raw, query_gain, key_gain, cotangent):
    tok_rows = query_raw.shape[0]
    head_size = query_raw.shape[2]
    full_width = query_raw.shape[1] * head_size * lax.axis_size("head")
    query_squares = jnp.sum(query_raw * query_raw, axis=(1, 2))
    key_squares = jnp.sum(key_raw * key_raw, axis=(1, 2))
    query_total, key_total = lax.psum((query_squares, key_squares), "head")
    query_scale = lax.rsqrt(query_total / full_width + epsilon)
    key_scale = lax.rsqrt(key_total / full_width + epsilon)
    query_unit = query_raw * query_scale[:, None, None]
    key_unit = key_raw * key_scale[:, None, None]
    query_hat = query_unit * query_gain[None]
    key_hat = key_unit * key_gain[None]
    tok_index = jnp.arange(tok_rows)
    position = (lax.axis_index("seq") * tok_rows + tok_index).astype(jnp.float32)
    position_weight = lax.rsqrt(float(head_size) * (position + 1.0))
    grad_scaled = cotangent * position_weight[:, None, None]
    local_state = product("thd,the->hde", key_hat, value_raw)
    local_grad = product("thd,the->hde", query_hat, grad_scaled)
    zero_state = jnp.zeros_like(local_state)
    earlier = carried_in(local_state, "seq", add_states, zero_state, False)
    later = carried_in(local_grad, "seq", add_states, zero_state, True)
    causal = tok_index[:, None] >= tok_index[None, :]
    scores = jnp.where(causal[None], product("thd,shd->hts", query_hat, key_hat), 0.0)
    attended = product("hts,she->the", scores, value_raw) + product(
        "thd,hde->the", query_hat, earlier
    )
    attended = attended * position_weight[:, None, None]
    mixing = jnp.where(causal[None], product("the,she->hts", grad_scaled, value_raw), 0.0)
    grad_qhat = product("hts,shd->thd", mixing, key_hat) + product(
        "the,hde->thd", grad_scaled, earlier
    )
    grad_khat = product("hts,thd->shd", mixing, query_hat) + product(
        "she,hde->shd", value_raw, later
    )
    grad_value = product("hts,the->she", scores, grad_scaled) + product(
        "shd,hde->she", key_hat, later
    )
    query_push = grad_qhat * query_gain[None]
    key_push = grad_khat * key_gain[None]
    query_along = jnp.sum(query_unit * query_push, axis=(1, 2))
    key_along = jnp.sum(key_unit * key_push, axis=(1, 2))
    query_inner, key_inner = lax.psum((query_along, key_along), "head")
    grad_query = query_scale[:, None, None] * (
        query_push - query_unit * (query_inner / full_width)[:, None, None]
    )
    grad_key = key_scale[:, None, None] * (
        key_push - key_unit * (key_inner / full_width)[:, None, None]
    )
    return (attended, grad_query, grad_key, grad_value)


def solution(mesh):
    return jax.shard_map(
        local,
        mesh=mesh,
        in_specs=(
            P("seq", "head", None),
            P("seq", "head", None),
            P("seq", "head", None),
            P("head", None),
            P("head", None),
            P("seq", "head", None),
        ),
        out_specs=(
            P("seq", "head", None),
            P("seq", "head", None),
            P("seq", "head", None),
            P("seq", "head", None),
        ),
        check_vma=False,
    )
```

profile of v0, /device:TPU:0, one launch (start us, length us, event | category | flops | bytes accessed | tf_op | source)
XLA Modules:
  0.0 124.6 jit_solution(1440770607640023506)
XLA Ops:
  7.2 0.0 copy-start
  7.2 0.0 copy-start.6
  7.2 0.0 copy-start.7
  7.2 0.0 all-gather.5.cloned.1.call-start
  7.2 1.3 %copy.30 = f32[256,4,128]{0,2,1:T(8,128)S(1)} copy(f32[256,4,128]{2,1,0:T(4,128)} %param.11) | data formatting | bytes 1048576 | tf_op args[1]
  8.6 0.0 copy-start.2
  8.6 0.0 copy-start.8
  8.6 2.3 %multiply_reduce_fusion.2 = (f32[256]{0:T(256)S(1)}, f32[256]{0:T(256)S(1)}) fusion(f32[256,4,128]{2,1,0:T(4,128)} %param.11, f32[256,4,128]{2,1,0:T(4,128)} %param.10), kind=kLoop, calls=%fused_computation.21 | loop fusion | flops 523776 | bytes 1050624 | tf_op jit(solution)/shard_map/reduce_sum | solution.py:37
  10.9 13.5 %all-reduce.1 = (f32[256]{0:T(256)S(1)}, f32[256]{0:T(256)S(1)}) all-reduce(f32[256]{0:T(256)S(1)} %get-tuple-element.117, f32[256]{0:T(256)S(1)} %get-tuple-element.118), channel_id=1, replica_groups=mesh['seq'=8,'head'=4] {'head'}, use_global_device_ids=true, to_apply=%region_3.0 | all-reduce | flops 512 | bytes 4096 | tf_op jit(solution)/shard_map/psum | solution.py:38
  24.4 0.0 copy-done
  24.4 0.0 copy-done.7
  24.4 1.4 %fusion.10 = f32[4,128,128]{2,1,0:T(8,128)} fusion(f32[256,4,128]{2,1,0:T(4,128)S(1)} %copy-done, f32[256,4,128]{0,2,1:T(8,128)S(1)} %copy.30, f32[4,128]{1,0:T(4,128)S(1)} %copy-done.7, f32[256]{0:T(256)S(1)} %add_rsqrt_fusion), kind=kOutput, calls=%fused_computation.28 | convolution fusion | flops 201588736 | bytes 1313792 | tf_op jit(solution)/shard_map/thd,the->hde/dot_general | solution.py:25
  25.8 0.0 all-gather.5.cloned.1.call-update
  25.8 0.0 all-gather.7.cloned.1.call-start
  25.9 0.2 copy.29
  26.2 0.0 copy-done.2
  26.2 0.0 copy-done.8
  26.2 1.5 %fusion.13 = f32[4,128,128]{2,1,0:T(8,128)} fusion(f32[256,4,128]{0,2,1:T(8,128)S(1)} %copy.29, f32[256,4,128]{2,1,0:T(4,128)S(1)} %copy-done.2, f32[256]{0:T(256)S(1)} %multiply_rsqrt_fusion, f32[4,128]{1,0:T(4,128)S(1)} %copy-done.8, f32[256]{0:T(256)S(1)} %add_rsqrt_fusion.1), kind=kOutput, calls=%fused_computation.31 | convolution fusion | flops 201719808 | bytes 1314816 | tf_op jit(solution)/shard_map/thd,the->hde/dot_general | solution.py:25
  27.6 0.0 all-gather.7.cloned.1.call-update
  27.7 2.0 %convolution_select_fusion = f32[4,256,256]{2,1,0:T(8,128)} fusion(pred[256,256]{1,0:T(8,128)(4,1)S(1)} %iota_compare_fusion, f32[256,4,128]{2,1,0:T(4,128)S(1)} %copy-done, f32[256,4,128]{2,1,0:T(4,128)S(1)} %copy-done.2, f32[256]{0:T(256)S(1)} %multiply_rsqrt_fusion), kind=kOutput, calls=%fused_computation.2 | convolution fusion | flops 403046400 | bytes 2163712 | tf_op jit(solution)/shard_map/the,she->hts/dot_general | solution.py:25
  29.7 1.3 %convolution_select_fusion.1 = f32[4,256,256]{2,1,0:T(8,128)S(1)} fusion(pred[256,256]{1,0:T(8,128)(4,1)S(1)} %iota_compare_fusion, f32[256,4,128]{0,2,1:T(8,128)S(1)} %copy.29, f32[256,4,128]{0,2,1:T(8,128)S(1)} %copy.30, f32[4,128]{1,0:T(4,128)S(1)} %copy-done.7, f32[256]{0:T(256)S(1)} %add_rsqrt_fusion, f32[4,128]{1,0:T(4,128)S(1)} %copy-done.8, ...), kind=kOutput, calls=%fused_computation.3 | convolution fusion | flops 403439616 | bytes 2168832 | tf_op jit(solution)/shard_map/thd,shd->hts/dot_general | solution.py:25
  31.0 21.0 %all-gather.5.cloned.1.call-done = f32[32,128,128]{2,1,0:T(8,128)} async-done(((f32[4,128,128]{2,1,0:T(8,128)}), f32[32,128,128]{2,1,0:T(8,128)}) %all-gather.5.cloned.1.call-update) | async-done | bytes 2097168 | tf_op jit(solution)/shard_map/all_gather | solution.py:14
  52.0 1.5 %fusion.15 = f32[4,128,256]{2,1,0:T(8,128)} fusion(f32[4,128,128]{2,1,0:T(8,128)S(1)} %get-tuple-element.83, f32[256,4,128]{2,1,0:T(4,128)S(1)} %copy-done.2, f32[256]{0:T(256)S(1)} %multiply_rsqrt_fusion), kind=kOutput, calls=%fused_computation.33 | convolution fusion | flops 201457664 | bytes 1311744 | tf_op jit(solution)/shard_map/the,hde->thd/dot_general | solution.py:25
  53.5 1.9 %convolution_bitcast_fusion = f32[256,4,128]{2,0,1:T(8,128)} fusion(f32[4,128,128]{2,1,0:T(8,128)S(1)} %get-tuple-element.83, f32[256,4,128]{0,2,1:T(8,128)S(1)} %copy.29, f32[4,128]{1,0:T(4,128)S(1)} %copy-done.8, f32[256]{0:T(256)S(1)} %add_rsqrt_fusion.1), kind=kOutput, calls=%fused_computation.12 | convolution fusion | flops 201588736 | bytes 1313792 | tf_op jit(solution)/shard_map/thd,hde->the/dot_general | solution.py:25
  55.4 26.8 %all-gather.7.cloned.1.call-done = f32[32,128,128]{2,1,0:T(8,128)} async-done(((f32[4,128,128]{2,1,0:T(8,128)}), f32[32,128,128]{2,1,0:T(8,128)}) %all-gather.7.cloned.1.call-update) | async-done | bytes 2097168 | tf_op jit(solution)/shard_map/all_gather | solution.py:14
  82.3 7.4 %while.23 = (s32[]{:T(128)}, f32[4,128,128]{2,1,0:T(8,128)S(1)}, s32[]{:T(128)}, f32[8,4,128,128]{3,2,1,0:T(8,128)}, s32[]{:T(128)}, /*index=5*/s32[]{:T(128)}, s32[]{:T(128)}, s32[]{:T(128)}) while((s32[]{:T(128)}, f32[4,128,128]{2,1,0:T(8,128)S(1)}, s32[]{:T(128)}, f32[8,4,128,128]{3,2,1,0:T(8,128)}, s32[]{:T(128)}, /*index=5*/s32[]{:T(128)}, ...), condition=%wide.region_9.10_spmd, body=%wide.region_8.9_spmd.sunk | while | flops 65542 | bytes 786575 | solution.py:21
  82.3 1.0 bitcast_add_fusion.5
  83.3 1.0 bitcast_add_fusion.5
  84.4 1.0 bitcast_add_fusion.5
  85.4 1.0 bitcast_add_fusion.5
  86.4 1.0 bitcast_add_fusion.5
  87.5 1.0 bitcast_add_fusion.5
  88.5 1.0 bitcast_add_fusion.5
  89.7 0.8 fusion.14
  90.5 0.0 copy-start.4
  90.5 1.4 %fusion.7 = f32[4,128,256]{2,1,0:T(8,128)} fusion(f32[4,128,128]{2,1,0:T(8,128)S(1)} %get-tuple-element.84, f32[256,4,128]{2,1,0:T(4,128)S(1)} %copy-done), kind=kOutput, calls=%fused_computation.25 | convolution fusion | flops 201326592 | bytes 1310720 | tf_op jit(solution)/shard_map/she,hde->shd/dot_general | solution.py:25
  91.9 1.9 %fusion = f32[256,4,128]{0,2,1:T(8,128)} fusion(f32[4,128,256]{2,1,0:T(8,128)S(1)} %fusion.14, f32[4,256,256]{2,1,0:T(8,128)S(1)} %convolution_select_fusion.1, f32[256,4,128]{2,1,0:T(4,128)S(1)} %copy-done.2, f32[256]{0:T(256)S(1)} %multiply_rsqrt_fusion), kind=kOutput, calls=%fused_computation.5 | convolution fusion | flops 402915328 | bytes 2622464 | tf_op jit(solution)/shard_map/hts,the->she/dot_general | solution.py:25
  93.8 1.1 fusion.6
  94.9 0.0 copy-start.1
  94.9 1.1 copy.44
  96.0 2.1 %copy.47 = f32[256,4,128]{2,1,0:T(4,128)} copy(f32[256,4,128]{0,2,1:T(8,128)} %fusion) | data formatting | bytes 1048576
  98.1 2.7 %multiply_reduce_fusion = (f32[256]{0:T(256)S(1)}, f32[256,4,128]{0,2,1:T(8,128)}) fusion(f32[256,4,128]{0,2,1:T(8,128)S(1)} %copy.30, f32[256]{0:T(256)S(1)} %add_rsqrt_fusion, f32[4,128]{1,0:T(4,128)S(1)} %copy-done.7, f32[4,128,256]{2,1,0:T(8,128)} %fusion.7, f32[4,256,256]{2,1,0:T(8,128)S(1)} %copy-done.1, f32[256,4,128]{0,2,1:T(8,128)S(1)} %copy.29, ...), kind=kOutput, calls=%fused_computation.18 | convolution fusion | flops 403570432 | bytes 3152896 | tf_op jit(solution)/shard_map/hts,thd->shd/dot_general | solution.py:25
  100.8 2.0 %multiply_reduce_fusion.1 = (f32[256]{0:T(256)S(1)}, f32[256,4,128]{0,2,1:T(8,128)}) fusion(f32[256,4,128]{0,2,1:T(8,128)S(1)} %copy.29, f32[256]{0:T(256)S(1)} %add_rsqrt_fusion.1, f32[4,128]{1,0:T(4,128)S(1)} %copy-done.8, f32[4,128,256]{2,1,0:T(8,128)S(1)} %copy-done.3, f32[4,256,256]{2,1,0:T(8,128)S(1)} %copy-done.1, f32[256,4,128]{0,2,1:T(8,128)S(1)} %copy.30, ...), kind=kOutput, calls=%fused_computation.20 | convolution fusion | flops 403570432 | bytes 3152896 | tf_op jit(solution)/shard_map/hts,shd->thd/dot_general | solution.py:25
  102.8 11.8 %all-reduce = (f32[256]{0:T(256)S(1)}, f32[256]{0:T(256)S(1)}) all-reduce(f32[256]{0:T(256)S(1)} %get-tuple-element.113, f32[256]{0:T(256)S(1)} %get-tuple-element.115), channel_id=1, replica_groups=mesh['seq'=8,'head'=4] {'head'}, use_global_device_ids=true, to_apply=%region_7.8 | all-reduce | flops 512 | bytes 4096 | tf_op jit(solution)/shard_map/psum | solution.py:74
  114.6 1.1 subtract_multiply_fusion.1
  115.7 1.0 copy.45
  116.7 0.1 subtract_multiply_fusion
  116.8 1.0 copy.46
  (16 shorter events, 0.1 us)
Async XLA Ops:
  7.2 17.2 %copy-start = (f32[256,4,128]{2,1,0:T(4,128)S(1)}, f32[256,4,128]{2,1,0:T(4,128)}, u32[]{:S(2)}) copy-start(f32[256,4,128]{2,1,0:T(4,128)} %param.12) | copy-start | bytes 1572868
  7.2 18.7 %copy-start.6 = (f32[256,4,128]{2,1,0:T(4,128)S(1)}, f32[256,4,128]{2,1,0:T(4,128)}, u32[]{:S(2)}) copy-start(f32[256,4,128]{2,1,0:T(4,128)} %param.10) | copy-start | bytes 1572868
  7.2 17.2 %copy-start.7 = (f32[4,128]{1,0:T(4,128)S(1)}, f32[4,128]{1,0:T(4,128)}, u32[]{:S(2)}) copy-start(f32[4,128]{1,0:T(4,128)} %param.14) | copy-start | bytes 6148
  7.2 44.8 %all-gather.5.cloned.1.call-start = ((), (), s32[]{:S(2)}) async-start(), calls=%async_computation | async-start | bytes 2359296 | tf_op jit(solution)/shard_map/all_gather | solution.py:14
  8.6 17.6 %copy-start.2 = (f32[256,4,128]{2,1,0:T(4,128)S(1)}, f32[256,4,128]{2,1,0:T(4,128)}, u32[]{:S(2)}) copy-start(f32[256,4,128]{2,1,0:T(4,128)} %param.15) | copy-start | bytes 1572868
  8.6 17.6 %copy-start.8 = (f32[4,128]{1,0:T(4,128)S(1)}, f32[4,128]{1,0:T(4,128)}, u32[]{:S(2)}) copy-start(f32[4,128]{1,0:T(4,128)} %param.13) | copy-start | bytes 6148
  25.8 56.4 %all-gather.7.cloned.1.call-start = ((), (), s32[]{:S(2)}) async-start(), calls=%async_computation.1 | async-start | bytes 2359296 | tf_op jit(solution)/shard_map/all_gather | solution.py:14
  90.5 3.3 %copy-start.4 = (f32[256,4,128]{2,0,1:T(8,128)S(1)}, f32[256,4,128]{2,0,1:T(8,128)}, u32[]{:S(2)}) copy-start(f32[256,4,128]{2,0,1:T(8,128)} %convolution_bitcast_fusion) | copy-start | bytes 1572868
  94.9 3.2 %copy-start.1 = (f32[4,256,256]{2,1,0:T(8,128)S(1)}, f32[4,256,256]{2,1,0:T(8,128)}, u32[]{:S(2)}) copy-start(f32[4,256,256]{2,1,0:T(8,128)} %convolution_select_fusion) | copy-start | bytes 3145732
  96.0 4.8 %copy-start.3 = (f32[4,128,256]{2,1,0:T(8,128)S(1)}, f32[4,128,256]{2,1,0:T(8,128)}, u32[]{:S(2)}) copy-start(f32[4,128,256]{2,1,0:T(8,128)} %fusion.15) | copy-start | bytes 1572868
  102.8 13.9 %copy-start.5 = (f32[256,4,128]{0,2,1:T(8,128)S(1)}, f32[256,4,128]{0,2,1:T(8,128)}, u32[]{:S(2)}) copy-start(f32[256,4,128]{0,2,1:T(8,128)} %get-tuple-element.116) | copy-start | bytes 1572868
Sparse Core Ops, SparseCore 0:
  26.0 25.9 all-gather.4
  54.4 27.7 all-gather.6
where the time goes:
time: 125 us
  waiting for transfers between devices  47.8 us (38%)
  blocking collectives  25.3 us (20%)
  matrix products  19.4 us (16%)
  between operations  14.2 us (11%)
  other arithmetic  10.6 us (8%)
  local copies, waits for them, and re-layouts  6.83 us (5%)
    all_gather x2, waiting for transfers between devices, carried_in(): gathered = lax.all_gather(part, axis)  47.8 us
    dot_general x12, matrix products, product(): jnp.einsum(form, left, right, precision=highest, preferred_element_type=j...  19.4 us
    psum x1, blocking collectives, local(): query_total, key_total = lax.psum((query_squares, key_squares), 'head')  13.5 us
    psum x1, blocking collectives, local(): query_inner, key_inner = lax.psum((query_along, key_along), 'head')  11.8 us
    add x7, other arithmetic, add_states(): return earlier + later  7.07 us
    unnamed x24, local copies, waits for them, and re-layouts  6.8 us
  transfers between devices with their start and end apart: 2, of which 2 were waited for; matrix products, arithmetic and copies ran while one was open for 7% of the time, Pallas kernels for 0%

commit v1 on v0

v1 whole, which is shorter than its diff:
```python
import functools

import jax
import jax.numpy as jnp
from jax import lax
from jax.experimental import pallas as pl
from jax.experimental.pallas import tpu as pltpu
from jax.sharding import PartitionSpec as P

epsilon = 1e-06
wide = jnp.float32
half_type = jnp.bfloat16
cores = 2
vmem_bytes = 12 * 1024 * 1024


def split(value):
    high = value.astype(half_type)
    low = (value - high.astype(wide)).astype(half_type)
    return high, low


def dot(left, right, left_dim=1, right_dim=0):
    return lax.dot_general(
        left, right, (((left_dim,), (right_dim,)), ((), ())), preferred_element_type=wide
    )


def row_sums(value):
    high, low = split(value)
    ones = jnp.ones((8, value.shape[1]), half_type)
    return (dot(ones, high, 1, 1) + dot(ones, low, 1, 1))[0:1]


def column_of(row):
    return jnp.transpose(jnp.broadcast_to(row, (8, row.shape[1])))[:, 0:1]


def head_rows(ref, head, heads):
    return ref[pl.ds(head, ref.shape[0] // heads, stride=heads), :]


def weight_column(place, tokens, head_size):
    index = lax.broadcasted_iota(jnp.int32, (tokens, head_size), 0)
    position = (place * tokens + index).astype(wide)
    return lax.rsqrt(float(head_size) * (position + 1.0))


def squares_kernel(heads, query_ref, key_ref, out_ref):
    for at, ref in enumerate((query_ref, key_ref)):
        total = None
        for head in range(heads):
            rows = head_rows(ref, head, heads)
            total = rows * rows if total is None else total + rows * rows
        out_ref[at : at + 1, :] = row_sums(total)


def prepare_kernel(
    heads, axis, query_ref, key_ref, value_ref, cot_ref, query_gain_ref, key_gain_ref,
    query_t_ref, key_t_ref, value_two_ref, cot_two_ref,
    score_high_ref, score_low_ref, mix_high_ref, mix_low_ref,
):
    tokens = query_ref.shape[0] // heads
    size = query_ref.shape[1]
    weight = weight_column(lax.axis_index(axis), tokens, size)
    causal = lax.broadcasted_iota(jnp.int32, (tokens, tokens), 0) >= lax.broadcasted_iota(
        jnp.int32, (tokens, tokens), 1
    )
    for head in range(heads):
        query = head_rows(query_ref, head, heads) * query_gain_ref[head : head + 1, :]
        key = head_rows(key_ref, head, heads) * key_gain_ref[head : head + 1, :]
        value = head_rows(value_ref, head, heads)
        cot = head_rows(cot_ref, head, heads) * weight
        query_t_ref[head] = jnp.transpose(query)
        key_t_ref[head] = jnp.transpose(key)
        for left, right, two_ref, high_ref, low_ref in (
            (query, key, None, score_high_ref, score_low_ref),
            (cot, value, None, mix_high_ref, mix_low_ref),
        ):
            left_high, left_low = split(left)
            right_high, right_low = split(right)
            if high_ref is mix_high_ref:
                cot_two_ref[head, :, :size] = left_high
                cot_two_ref[head, :, size:] = left_low
                value_two_ref[head, :, :size] = right_high
                value_two_ref[head, :, size:] = right_low
            product = dot(
                jnp.concatenate([left_high, left_low], 1),
                jnp.concatenate([right_high, right_high], 1), 1, 1,
            ) + dot(left_high, right_low, 1, 1)
            high, low = split(jnp.where(causal, product, 0.0))
            high_ref[head] = high
            low_ref[head] = low


def states_kernel(heads, width, *refs):
    *part_refs, query_t_ref, key_t_ref, value_two_ref, cot_two_ref, scale_ref, state_ref, grad_ref = refs
    size = query_t_ref.shape[1]
    total = part_refs[0][...]
    for ref in part_refs[1:]:
        total = total + ref[...]
    scale = lax.rsqrt(total * (1.0 / width) + epsilon)
    scale_ref[...] = scale
    for raw_ref, row, other_ref, out_ref in (
        (key_t_ref, scale[1:2], value_two_ref, state_ref),
        (query_t_ref, scale[0:1], cot_two_ref, grad_ref),
    ):
        for head in range(heads):
            high, low = split(raw_ref[head] * row)
            pair = dot(jnp.concatenate([high, low], 0), other_ref[head])
            out_ref[head * size : (head + 1) * size, :] = (
                pair[:size, :size] + pair[:size, size:] + pair[size:, :size]
            )


def intra_kernel(
    heads, scale_ref, query_ref, key_ref, query_gain_ref, key_gain_ref, value_two_ref, cot_two_ref,
    score_high_ref, score_low_ref, mix_high_ref, mix_low_ref,
    query_two_ref, key_two_ref, attended_ref, grad_query_ref, grad_key_ref, grad_value_ref,
):
    size = query_ref.shape[1]
    query_scale = column_of(scale_ref[0:1, :])
    key_scale = column_of(scale_ref[1:2, :])

    def by_two(high, low, right, transposed):
        right_high, right_low = split(right)
        dim = 0 if transposed else 1
        both = dot(high, jnp.concatenate([right_high, right_low], 1), dim, 0)
        return both[:, :size] + both[:, size:] + dot(low, right_high, dim, 0)

    for head in range(heads):
        query = head_rows(query_ref, head, heads) * query_gain_ref[head : head + 1, :] * query_scale
        key = head_rows(key_ref, head, heads) * key_gain_ref[head : head + 1, :] * key_scale
        value = value_two_ref[head, :, :size].astype(wide) + value_two_ref[head, :, size:].astype(wide)
        cot = cot_two_ref[head, :, :size].astype(wide) + cot_two_ref[head, :, size:].astype(wide)
        for source, ref in ((query, query_two_ref), (key, key_two_ref)):
            high, low = split(source)
            ref[head, :, :size] = high
            ref[head, :, size:] = low
        score_high, score_low = score_high_ref[head], score_low_ref[head]
        mix_high, mix_low = mix_high_ref[head], mix_low_ref[head]
        attended_ref[head] = by_two(score_high, score_low, value * key_scale, False) * query_scale
        grad_value_ref[head] = by_two(score_high, score_low, cot * query_scale, True) * key_scale
        grad_query_ref[head] = by_two(mix_high, mix_low, key, False)
        grad_key_ref[head] = by_two(mix_high, mix_low, query, True)


def outputs_kernel(
    heads, axis, earlier_ref, later_ref, query_two_ref, key_two_ref, attended_in_ref, grad_value_in_ref,
    value_ref, cot_ref, attended_ref, grad_value_ref, inner_ref,
):
    tokens = value_ref.shape[0] // heads
    size = value_ref.shape[1]
    weight = weight_column(lax.axis_index(axis), tokens, size)
    blank = jnp.zeros((size, size), half_type)
    for at, (state_ref, two_ref, intra_ref, other_ref, out_ref) in enumerate((
        (earlier_ref, query_two_ref, attended_in_ref, cot_ref, attended_ref),
        (later_ref, key_two_ref, grad_value_in_ref, value_ref, grad_value_ref),
    )):
        inner = None
        for head in range(heads):
            high, low = split(state_ref[head * size : (head + 1) * size, :])
            right = jnp.concatenate(
                [jnp.concatenate([high, low], 1), jnp.concatenate([high, blank], 1)], 0
            )
            both = dot(two_ref[head], right)
            result = both[:, :size] + both[:, size:] + intra_ref[head]
            if at == 0:
                result = result * weight
            out_ref[pl.ds(head, tokens, stride=heads), :] = result
            term = result * head_rows(other_ref, head, heads)
            inner = term if inner is None else inner + term
        inner_ref[at : at + 1, :] = row_sums(inner)


def pushes_kernel(
    heads, scale_ref, earlier_ref, later_ref, cot_two_ref, value_two_ref, grad_query_ref, grad_key_ref,
    query_gain_ref, key_gain_ref, query_push_ref, key_push_ref,
):
    tokens = cot_two_ref.shape[1]
    size = query_gain_ref.shape[1]
    blank = jnp.zeros((size, size), half_type)
    for at, (state_ref, two_ref, intra_ref, gain_ref, out_ref) in enumerate((
        (earlier_ref, cot_two_ref, grad_query_ref, query_gain_ref, query_push_ref),
        (later_ref, value_two_ref, grad_key_ref, key_gain_ref, key_push_ref),
    )):
        scale = column_of(scale_ref[at : at + 1, :])
        for head in range(heads):
            high, low = split(state_ref[head * size : (head + 1) * size, :])
            right = jnp.concatenate(
                [jnp.concatenate([high, high], 1), jnp.concatenate([low, blank], 1)], 0
            )
            both = dot(two_ref[head], right, 1, 1)
            result = (both[:, :size] + both[:, size:] + intra_ref[head]) * gain_ref[head : head + 1, :]
            out_ref[pl.ds(head, tokens, stride=heads), :] = result * scale


def final_kernel(heads, width, *refs):
    *part_refs, scale_ref, query_ref, key_ref, query_push_ref, key_push_ref, query_out_ref, key_out_ref = refs
    tokens = query_ref.shape[0] // heads
    total = part_refs[0][...]
    for ref in part_refs[1:]:
        total = total + ref[...]
    factor = scale_ref[...] * scale_ref[...] * total * (1.0 / width)
    for at, (raw_ref, push_ref, out_ref) in enumerate((
        (query_ref, query_push_ref, query_out_ref),
        (key_ref, key_push_ref, key_out_ref),
    )):
        column = column_of(factor[at : at + 1])
        for head in range(heads):
            out_ref[pl.ds(head, tokens, stride=heads), :] = head_rows(
                push_ref, head, heads
            ) - head_rows(raw_ref, head, heads) * column


def call(kernel, outs, args, flops, name):
    whole = pl.BlockSpec(memory_space=pltpu.VMEM)
    shapes = [jax.ShapeDtypeStruct(shape, kind) for shape, kind in outs]
    moved = sum(a.size * a.dtype.itemsize for a in (*args, *shapes))
    return pl.pallas_call(
        kernel,
        out_shape=shapes,
        in_specs=[whole] * len(args),
        out_specs=[whole] * len(shapes),
        compiler_params=pltpu.CompilerParams(vmem_limit_bytes=vmem_bytes),
        cost_estimate=pl.CostEstimate(flops=int(flops), bytes_accessed=int(moved), transcendentals=0),
        name=name,
    )(*args)


def from_others(part, axis):
    count = lax.axis_size(axis)
    paired = count & (count - 1) == 0
    parts = [part]
    for step in range(count - 1, 0, -1):
        pairs = [(at, at ^ step if paired else (at + step) % count) for at in range(count)]
        parts.append(lax.ppermute(part, axis, pairs))
    return parts


def radices(count):
    out = []
    while count % 4 == 0 and count > 1:
        out.append(4)
        count //= 4
    divisor = 2
    while count > 1:
        while count % divisor == 0:
            out.append(divisor)
            count //= divisor
        divisor += 1
    return out


def neighbour_states(state, grad, axis):
    count = lax.axis_size(axis)
    place = lax.axis_index(axis)
    swap = [(at, at ^ 1) for at in range(count)]
    core = place % cores
    other_state = lax.ppermute(state, axis, swap)
    other_grad = lax.ppermute(grad, axis, swap)
    rows = state.shape[0] // cores

    def mine(value):
        return lax.dynamic_slice_in_dim(value, core * rows, rows, 0)

    up = mine(state) + mine(other_state)
    down = mine(grad) + mine(other_grad)
    earlier = jnp.zeros_like(up)
    later = jnp.zeros_like(down)
    stride = cores
    steps = radices(count // cores)
    for level, radix in enumerate(steps):
        last = level == len(steps) - 1
        paired = radix & (radix - 1) == 0
        digit = place // stride % radix
        got = []
        for step in range(1, radix):
            pairs = []
            for at in range(count):
                own = at // stride % radix
                goal = own ^ step if paired else (own + step) % radix
                pairs.append((at, at + (goal - own) * stride))
            target = digit ^ step if paired else (digit + step) % radix
            source = digit ^ step if paired else (digit + radix - step) % radix
            if last:
                message = jnp.where(target > digit, up, down)
            else:
                message = jnp.concatenate([up, down], 0)
            got.append((source, lax.ppermute(message, axis, pairs)))
        for source, message in got:
            first, second = (message, message) if last else (message[:rows], message[rows:])
            earlier = earlier + jnp.where(source < digit, first, 0.0)
            later = later + jnp.where(source > digit, second, 0.0)
            if not last:
                up = up + first
                down = down + second
        stride *= radix
    both = jnp.concatenate([earlier, later], 0)
    shared = lax.ppermute(both, axis, swap)

    def whole(own, shared_part):
        return jnp.where(
            core == 0,
            jnp.concatenate([own, shared_part], 0),
            jnp.concatenate([shared_part, own], 0),
        )

    return (
        whole(earlier, shared[:rows]) + jnp.where(core == 1, other_state, 0.0),
        whole(later, shared[rows:]) + jnp.where(core == 0, other_grad, 0.0),
    )


def local(query_raw, key_raw, value_raw, query_gain, key_gain, cotangent):
    tokens, heads, size = query_raw.shape
    width = float(heads * size * lax.axis_size("head"))
    query, key, value, cot = (
        a.reshape(tokens * heads, size) for a in (query_raw, key_raw, value_raw, cotangent)
    )
    rows = ((2, tokens), wide)
    flat = ((tokens * heads, size), wide)
    square = ((heads, tokens, tokens), half_type)
    twice = ((heads, tokens, 2 * size), half_type)
    turned = ((heads, size, tokens), wide)
    stack = ((heads, tokens, size), wide)
    state_shape = ((heads * size, size), wide)
    work = 2 * heads * tokens * tokens * size

    (squares,) = call(functools.partial(squares_kernel, heads), [rows], [query, key], work / 8, "squares")
    parts = from_others(squares, "head")
    query_t, key_t, value_two, cot_two, *grids = call(
        functools.partial(prepare_kernel, heads, "seq"),
        [turned, turned, twice, twice, square, square, square, square],
        [query, key, value, cot, query_gain, key_gain], 6 * work, "prepare",
    )
    scale, state, grad = call(
        functools.partial(states_kernel, heads, width), [rows, state_shape, state_shape],
        [*parts, query_t, key_t, value_two, cot_two], 4 * work, "states",
    )
    query_two, key_two, attended_in, grad_query_in, grad_key_in, grad_value_in = call(
        functools.partial(intra_kernel, heads),
        [twice, twice, stack, stack, stack, stack],
        [scale, query, key, query_gain, key_gain, value_two, cot_two, *grids], 12 * work, "intra",
    )
    earlier, later = neighbour_states(state, grad, "seq")
    attended, grad_value, inner = call(
        functools.partial(outputs_kernel, heads, "seq"), [flat, flat, rows],
        [earlier, later, query_two, key_two, attended_in, grad_value_in, value, cot], 4 * work, "outputs",
    )
    inners = from_others(inner, "head")
    query_push, key_push = call(
        functools.partial(pushes_kernel, heads), [flat, flat],
        [scale, earlier, later, cot_two, value_two, grad_query_in, grad_key_in, query_gain, key_gain],
        4 * work, "pushes",
    )
    grad_query, grad_key = call(
        functools.partial(final_kernel, heads, width), [flat, flat],
        [*inners, scale, query, key, query_push, key_push], work / 8, "final",
    )
    return tuple(
        a.reshape(tokens, heads, size) for a in (attended, grad_query, grad_key, grad_value)
    )


def solution(mesh):
    tensor = P("seq", "head", None)
    gain = P("head", None)
    return jax.shard_map(
        local,
        mesh=mesh,
        in_specs=(tensor, tensor, tensor, gain, gain, tensor),
        out_specs=(tensor,) * 4,
        check_vma=False,
    )
```

time: 125 us -> 47.2 us (0.38)
  waiting for transfers between devices: 47.8 us -> 13.1 us
  blocking collectives: 25.3 us -> 0 us
  matrix products: 19.4 us -> 0 us
  starting transfers between devices: 0.08 us -> 14.1 us
  between operations: 14.2 us -> 0.82 us
  other arithmetic: 10.6 us -> 3.26 us
  Pallas kernels: 0 us -> 6.62 us
  local copies, waits for them, and re-layouts: 6.83 us -> 8.83 us
    all_gather x2 -> x0, waiting for transfers between devices: 47.8 us -> none  [carried_in(): gathered = lax.all_gather(part, axis)]
    psum x2 -> x0, blocking collectives: 25.3 us -> none  [the longest x1 13.5 us: local(): query_total, key_total = lax.psum((query_squares, key_squares), 'head')]
    dot_general x12 -> x0, matrix products: 19.4 us -> none  [product(): jnp.einsum(form, left, right, precision=highest, preferred_element_type=j...]
    ppermute x0 -> x12, starting transfers between devices: none -> 14.1 us  [the longest x6 10.1 us: from_others(): parts.append(lax.ppermute(part, axis, pairs))]
    ppermute x0 -> x12, waiting for transfers between devices: none -> 13.1 us  [the longest x3 6.28 us: neighbour_states(): got.append((source, lax.ppermute(message, axis, pairs)))]
    pallas_call x0 -> x7, Pallas kernels: none -> 6.62 us  [call(): pl.pallas_call(kernel, out_shape=shapes, in_specs=[whole] * len(args), ou...]
    add x7 -> x2, other arithmetic: 7.07 us -> 1.09 us  [the longest x1 1.03 us: neighbour_states(): later = later + jnp.where(source > digit, second, 0.0)]
    reduce_sum x1 -> x0, other arithmetic: 2.29 us -> none  [local(): key_squares = jnp.sum(key_raw * key_raw, axis=(1, 2))]
  transfers between devices with their start and end apart: 2 -> 12, of which waited for: 2 -> 7; matrix products, arithmetic and copies ran while one was open for 7% -> 2% of each run, Pallas kernels for 0% -> 7%
where the time goes in v1:
time: 47.2 us; the launch traced here: 46.7 us
  starting transfers between devices  14.1 us (30%)
  waiting for transfers between devices  13.1 us (28%)
  local copies, waits for them, and re-layouts  8.83 us (19%)
  Pallas kernels  6.62 us (14%)
  other arithmetic  3.26 us (7%)
  between operations  0.82 us (2%)
    ppermute x6, starting transfers between devices, from_others(): parts.append(lax.ppermute(part, axis, pairs))  10.1 us
    unnamed x42, local copies, waits for them, and re-layouts  7.79 us
    pallas_call x7, Pallas kernels, call(): pl.pallas_call(kernel, out_shape=shapes, in_specs=[whole] * len(args), ou...  6.62 us
    ppermute x3, waiting for transfers between devices, neighbour_states(): got.append((source, lax.ppermute(message, axis, pairs)))  6.28 us
    ppermute x6, waiting for transfers between devices, from_others(): parts.append(lax.ppermute(part, axis, pairs))  5.38 us
    ppermute x3, starting transfers between devices, neighbour_states(): got.append((source, lax.ppermute(message, axis, pairs)))  3.49 us
    select_n x2, other arithmetic, neighbour_states(): message = jnp.where(target > digit, up, down)  1.44 us
    slice x1, local copies, waits for them, and re-layouts, neighbour_states(): shared[rows:]  1.04 us
  transfers between devices with their start and end apart: 12, of which 7 were waited for; matrix products, arithmetic and copies ran while one was open for 2% of the time, Pallas kernels for 7%

profile of v1, /device:TPU:0, one launch (start us, length us, event | category | flops | bytes accessed | tf_op | source)
XLA Modules:
  0.0 46.7 jit_solution(7616018477021625343)
XLA Ops:
  0.6 0.0 copy-start
  0.6 1.0 %copy-done = f32[256,4,128]{2,1,0:T(4,128)S(1)} copy-done((f32[256,4,128]{2,1,0:T(4,128)S(1)}, f32[256,4,128]{2,1,0:T(4,128)}, u32[]{:S(2)}) %copy-start) | copy-done | bytes 524312
  1.7 1.0 %copy-done.2 = f32[256,4,128]{2,1,0:T(4,128)S(1)} copy-done((f32[256,4,128]{2,1,0:T(4,128)S(1)}, f32[256,4,128]{2,1,0:T(4,128)}, u32[]{:S(2)}) %copy-start.2) | copy-done | bytes 524312
  2.7 0.2 squares.1.refs_0_
  3.0 3.1 %collective-permute-start.2 = (f32[2,256]{1,0:T(2,128)S(1)}, f32[2,256]{1,0:T(2,128)S(1)}, u32[]{:S(2)}, u32[]{:S(2)}) collective-permute-start(f32[2,256]{1,0:T(2,128)S(1)} %squares.1.refs_0_), channel_id=1, source_target_pairs={{0,1},{1,0},{2,3},{3,2},{4,5},{5,4},{6,7},{7,6},{8,9},{9,8},{10,11... | collective-permute-start | bytes 6152 | tf_op jit(solution)/shard_map/ppermute | solution.py:237
  6.0 2.6 %collective-permute-start.1 = (f32[2,256]{1,0:T(2,128)S(1)}, f32[2,256]{1,0:T(2,128)S(1)}, u32[]{:S(2)}, u32[]{:S(2)}) collective-permute-start(f32[2,256]{1,0:T(2,128)S(1)} %squares.1.refs_0_), channel_id=1, source_target_pairs={{0,2},{1,3},{2,0},{3,1},{4,6},{5,7},{6,4},{7,5},{8,10},{9,11},{10,... | collective-permute-start | bytes 6152 | tf_op jit(solution)/shard_map/ppermute | solution.py:237
  8.6 0.0 collective-permute-start
  8.7 0.9 %prepare.1 = (f32[4,128,256]{2,1,0:T(8,128)S(1)}, f32[4,128,256]{2,1,0:T(8,128)S(1)}, bf16[4,256,256]{2,1,0:T(8,128)(2,1)S(1)}, bf16[4,256,256]{2,1,0:T(8,128)(2...) custom-call(f32[1024,128]{1,0:T(8,128)S(1)} %bitcast.9, ...), custom_call_target="tpu_custom_call" | custom-call | flops 402653184 | bytes 6295552 | tf_op jit(solution)/shard_map/prepare/pallas_call | solution.py:220
  9.5 0.0 copy-start.6
  9.5 0.8 %copy-done.6 = bf16[4,256,256]{2,1,0:T(8,128)(2,1)} copy-done((bf16[4,256,256]{2,1,0:T(8,128)(2,1)}, bf16[4,256,256]{2,1,0:T(8,128)(2,1)S(1)}, u32[]{:S(2)}) %copy-start.6) | copy-done | bytes 524312
  10.3 0.0 collective-permute-done.2.refs_3_
  10.3 0.2 collective-permute-done.1.refs_2_
  10.5 3.5 %collective-permute-done.refs_1_ = f32[2,256]{1,0:T(2,128)S(1)} collective-permute-done((f32[2,256]{1,0:T(2,128)S(1)}, f32[2,256]{1,0:T(2,128)S(1)}, u32[]{:S(2)}, u32[]{:S(2)}) %collective-permute-start) | collective-permute-done | bytes 2080 | tf_op jit(solution)/shard_map/ppermute | solution.py:237
  14.0 0.4 states.1
  14.5 0.1 collective-permute-start.3
  14.6 0.5 %collective-permute-start.4 = (f32[512,128]{1,0:T(8,128)S(1)}, f32[512,128]{1,0:T(8,128)S(1)}, u32[]{:S(2)}, u32[]{:S(2)}) collective-permute-start(f32[512,128]{1,0:T(8,128)S(1)} %get-tuple-element.33), channel_id=1, source_target_pairs={{0,4},{4,0},{8,12},{12,8},{16,20},{20,16},{24,28},{28,24},{1,5},{5... | collective-permute-start | bytes 786440 | tf_op jit(solution)/shard_map/ppermute | solution.py:261
  15.1 1.0 %collective-permute-done.3 = f32[512,128]{1,0:T(8,128)S(1)} collective-permute-done((f32[512,128]{1,0:T(8,128)S(1)}, f32[512,128]{1,0:T(8,128)S(1)}, u32[]{:S(2)}, u32[]{:S(2)}) %collective-permute-start.3) | collective-permute-done | bytes 262176 | tf_op jit(solution)/shard_map/ppermute | solution.py:260
  16.1 0.4 collective-permute-done.4
  16.5 0.7 %broadcast_select_fusion.2 = (f32[256,128]{1,0:T(8,128)}, f32[256,128]{1,0:T(8,128)S(1)}, f32[256,128]{1,0:T(8,128)S(1)}) fusion(pred[]{:T(512)S(6)} %gt.12, f32[512,128]{1,0:T(8,128)S(1)} %collective-permute-done.4, s32[]{:T(128)S(6)} %select_n.103, f32[512,128]{1,0:T(8,128)S(1)} %get-tuple-element.33, f32[512,128]{1,0:T(8,128)S(1)} %collective-permute-done.3, ...), kind=kLoop, calls=%fused_computation.13 | loop fusion | flops 98304 | bytes 917509 | tf_op jit(solution)/shard_map/jit(_where)/select_n | solution.py:287
  17.2 1.5 %collective-permute-start.5 = (f32[256,128]{1,0:T(8,128)}, f32[256,128]{1,0:T(8,128)S(1)}, u32[]{:S(2)}, u32[]{:S(2)}) collective-permute-start(f32[256,128]{1,0:T(8,128)} %get-tuple-element.52), channel_id=1, source_target_pairs={{0,8},{4,12},{8,0},{12,4},{16,24},{20,28},{24,16},{28,20},{1,9},{5... | collective-permute-start | bytes 393224 | tf_op jit(solution)/shard_map/ppermute | solution.py:290
  18.7 0.7 %broadcast_select_fusion.1 = (f32[256,128]{1,0:T(8,128)}, f32[256,128]{1,0:T(8,128)}) fusion(f32[256,128]{1,0:T(8,128)S(1)} %get-tuple-element.54, f32[256,128]{1,0:T(8,128)S(1)} %get-tuple-element.53, pred[]{:T(512)S(6)} %gt.13, pred[]{:T(512)S(6)} %gt.14), kind=kLoop, calls=%fused_computation.12 | loop fusion | flops 65536 | bytes 524290 | tf_op jit(solution)/shard_map/jit(_where)/select_n | solution.py:287
  19.4 1.5 %collective-permute-start.6 = (f32[256,128]{1,0:T(8,128)}, f32[256,128]{1,0:T(8,128)S(1)}, u32[]{:S(2)}, u32[]{:S(2)}) collective-permute-start(f32[256,128]{1,0:T(8,128)} %get-tuple-element.59), channel_id=1, source_target_pairs={{0,16},{4,20},{8,24},{12,28},{16,0},{20,4},{24,8},{28,12},{1,17},{... | collective-permute-start | bytes 393224 | tf_op jit(solution)/shard_map/ppermute | solution.py:290
  20.9 0.5 %collective-permute-start.7 = (f32[256,128]{1,0:T(8,128)}, f32[256,128]{1,0:T(8,128)}, u32[]{:S(2)}, u32[]{:S(2)}) collective-permute-start(f32[256,128]{1,0:T(8,128)} %get-tuple-element.60), channel_id=1, source_target_pairs={{0,24},{4,28},{8,16},{12,20},{16,8},{20,12},{24,0},{28,4},{1,25},{... | collective-permute-start | bytes 393224 | tf_op jit(solution)/shard_map/ppermute | solution.py:290
  21.4 1.5 %collective-permute-done.5 = f32[256,128]{1,0:T(8,128)S(1)} collective-permute-done((f32[256,128]{1,0:T(8,128)}, f32[256,128]{1,0:T(8,128)S(1)}, u32[]{:S(2)}, u32[]{:S(2)}) %collective-permute-start.5) | collective-permute-done | bytes 131104 | tf_op jit(solution)/shard_map/ppermute | solution.py:290
  23.0 4.7 %collective-permute-done.6 = f32[256,128]{1,0:T(8,128)S(1)} collective-permute-done((f32[256,128]{1,0:T(8,128)}, f32[256,128]{1,0:T(8,128)S(1)}, u32[]{:S(2)}, u32[]{:S(2)}) %collective-permute-start.6) | collective-permute-done | bytes 131104 | tf_op jit(solution)/shard_map/ppermute | solution.py:290
  27.7 0.6 %copy-done.20 = f32[256,128]{1,0:T(8,128)} copy-done((f32[256,128]{1,0:T(8,128)}, f32[256,128]{1,0:T(8,128)S(1)}, u32[]{:S(2)}) %copy-start.20) | copy-done | bytes 131096
  28.3 0.0 collective-permute-done.7
  28.3 1.0 %select_add_fusion = (f32[256,128]{1,0:T(8,128)S(1)}, f32[256,128]{1,0:T(8,128)S(1)}) fusion(f32[256,128]{1,0:T(8,128)} %collective-permute-done.7, f32[256,128]{1,0:T(8,128)} %copy-done.20, f32[256,128]{1,0:T(8,128)S(1)} %collective-permute-done.5, pred[]{:T(512)S(6)} %gt.14, pred[]{:T(512)S(6)} %gt.13, pred[]{:T(512)S(6)} %gt.12, pred[]{:T(512)S(6)} %lt.30, ...), kind=kLoop, calls=%fused_computation.7 | loop fusion | flops 327680 | bytes 655366 | tf_op jit(solution)/shard_map/add | solution.py:294
  29.4 0.7 %pad_maximum_fusion.1 = f32[512,128]{1,0:T(8,128)} fusion(f32[256,128]{1,0:T(8,128)S(1)} %get-tuple-element.55, f32[256,128]{1,0:T(8,128)S(1)} %get-tuple-element.56), kind=kLoop, calls=%fused_computation.1 | loop fusion | flops 65536 | bytes 524288 | tf_op jit(solution)/shard_map/concatenate | solution.py:299
  30.1 0.0 collective-permute-start.8
  30.1 0.0 copy-start.7
  30.1 1.0 %copy-done.7 = bf16[4,256,256]{2,1,0:T(8,128)(2,1)S(1)} copy-done((bf16[4,256,256]{2,1,0:T(8,128)(2,1)S(1)}, bf16[4,256,256]{2,1,0:T(8,128)(2,1)}, u32[]{:S(2)}) %copy-start.7) | copy-done | bytes 524312
  31.1 1.0 %copy-done.9 = bf16[4,256,256]{2,1,0:T(8,128)(2,1)S(1)} copy-done((bf16[4,256,256]{2,1,0:T(8,128)(2,1)S(1)}, bf16[4,256,256]{2,1,0:T(8,128)(2,1)}, u32[]{:S(2)}) %copy-start.9) | copy-done | bytes 524312
  32.2 1.0 %copy-done.11 = bf16[4,256,256]{2,1,0:T(8,128)(2,1)S(1)} copy-done((bf16[4,256,256]{2,1,0:T(8,128)(2,1)S(1)}, bf16[4,256,256]{2,1,0:T(8,128)(2,1)}, u32[]{:S(2)}) %copy-start.11) | copy-done | bytes 524312
  33.2 1.0 %copy-done.13 = bf16[4,256,256]{2,1,0:T(8,128)(2,1)S(1)} copy-done((bf16[4,256,256]{2,1,0:T(8,128)(2,1)S(1)}, bf16[4,256,256]{2,1,0:T(8,128)(2,1)}, u32[]{:S(2)}) %copy-start.13) | copy-done | bytes 524312
  34.3 1.7 %intra.1 = (bf16[4,256,256]{2,1,0:T(8,128)(2,1)S(1)}, bf16[4,256,256]{2,1,0:T(8,128)(2,1)S(1)}, f32[4,256,128]{2,1,0:T(8,128)S(1)}, f32[4,256,128]{2,1,0:T(8,128...) custom-call(f32[2,256]{1,0:T(2,128)S(1)} %get-tuple-element.34.scale_ref.refs_4_, ...), custom_call_target="tpu_custom_call" | custom-call | flops 805306368 | bytes 7346176 | tf_op jit(solution)/shard_map/intra/pallas_call | solution.py:220
  36.0 0.0 collective-permute-done.8
  36.0 1.0 %fusion.4 = (f32[256,128]{1,0:T(8,128)S(1)}, f32[256,128]{1,0:T(8,128)S(1)}) fusion(f32[512,128]{1,0:T(8,128)} %collective-permute-done.8), kind=kLoop, calls=%fused_computation.14 | loop fusion | bytes 524288 | tf_op jit(solution)/shard_map/slice | solution.py:311
  37.0 0.1 copy-done.19
  37.1 0.1 fusion.1
  37.2 1.6 %outputs.1 = (f32[1024,128]{1,0:T(8,128)}, f32[1024,128]{1,0:T(8,128)}, f32[2,256]{1,0:T(2,128)S(1)}) custom-call(f32[512,128]{1,0:T(8,128)S(1)} %get-tuple-element.61.earlier_ref, f32[512,128]{1,0:T(8,128)S(1)} %get-tuple-element.62.later_ref, bf16[4,256,256]{2,1,0:T(8,128)(2,1)S(1)} %get-tuple-element.39.query_two_ref, ...), custom_call_target="tpu_custom_call" | custom-call | flops 268435456 | bytes 4720640 | tf_op jit(solution)/shard_map/outputs/pallas_call | solution.py:220
  38.8 0.0 collective-permute-start.11
  38.8 1.3 %collective-permute-start.10 = (f32[2,256]{1,0:T(2,128)S(1)}, f32[2,256]{1,0:T(2,128)S(1)}, u32[]{:S(2)}, u32[]{:S(2)}) collective-permute-start(f32[2,256]{1,0:T(2,128)S(1)} %get-tuple-element.44.refs_0_), channel_id=1, source_target_pairs={{0,2},{1,3},{2,0},{3,1},{4,6},{5,7},{6,4},{7,5},{8,10},{9,11},{10,... | collective-permute-start | bytes 6152 | tf_op jit(solution)/shard_map/ppermute | solution.py:237
  40.1 3.1 %collective-permute-start.9 = (f32[2,256]{1,0:T(2,128)S(1)}, f32[2,256]{1,0:T(2,128)S(1)}, u32[]{:S(2)}, u32[]{:S(2)}) collective-permute-start(f32[2,256]{1,0:T(2,128)S(1)} %get-tuple-element.44.refs_0_), channel_id=1, source_target_pairs={{0,3},{1,2},{2,1},{3,0},{4,7},{5,6},{6,5},{7,4},{8,11},{9,10},{10,... | collective-permute-start | bytes 6152 | tf_op jit(solution)/shard_map/ppermute | solution.py:237
  43.2 0.5 %pushes.1 = (f32[1024,128]{1,0:T(8,128)S(1)}, f32[1024,128]{1,0:T(8,128)S(1)}) custom-call(f32[2,256]{1,0:T(2,128)S(1)} %get-tuple-element.34.scale_ref.refs_4_, f32[512,128]{1,0:T(8,128)S(1)} %get-tuple-element.61.earlier_ref, f32[512,128]{1,0:T(8,128)S(1)} %get-tuple-element.62.later_ref, bf16[4,256,256]{2,1,0:T(8,128)(2,1)S(1)} %get-tuple-element.31.refs_7_.cot_two_ref, ...), custom_call_target="tpu_custom_call" | custom-call | flops 268435456 | bytes 3676160 | tf_op jit(solution)/shard_map/pushes/pallas_call | solution.py:220
  43.7 0.0 collective-permute-done.11.refs_3_
  43.8 1.7 %collective-permute-done.9.refs_1_ = f32[2,256]{1,0:T(2,128)S(1)} collective-permute-done((f32[2,256]{1,0:T(2,128)S(1)}, f32[2,256]{1,0:T(2,128)S(1)}, u32[]{:S(2)}, u32[]{:S(2)}) %collective-permute-start.9) | collective-permute-done | bytes 2080 | tf_op jit(solution)/shard_map/ppermute | solution.py:237
  45.5 1.2 %final.1 = (f32[1024,128]{1,0:T(8,128)}, f32[1024,128]{1,0:T(8,128)}) custom-call(f32[2,256]{1,0:T(2,128)S(1)} %get-tuple-element.44.refs_0_, f32[2,256]{1,0:T(2,128)S(1)} %collective-permute-done.9.refs_1_, f32[2,256]{1,0:T(2,128)S(1)} %collective-permute-done.10.refs_2_, f32[2,256]{1,0:T(2,128)S(1)} %collective-permute-done.11.refs_3_, ...), custom_call_target="tpu_custom_call" | custom-call | flops 8388608 | bytes 3155968 | tf_op jit(solution)/shard_map/final/pallas_call | solution.py:220
  (31 shorter events, 0.1 us)
Async XLA Ops:
  0.6 1.0 %copy-start = (f32[256,4,128]{2,1,0:T(4,128)S(1)}, f32[256,4,128]{2,1,0:T(4,128)}, u32[]{:S(2)}) copy-start(f32[256,4,128]{2,1,0:T(4,128)} %param.6) | copy-start | bytes 1572868
  1.7 1.0 %copy-start.2 = (f32[256,4,128]{2,1,0:T(4,128)S(1)}, f32[256,4,128]{2,1,0:T(4,128)}, u32[]{:S(2)}) copy-start(f32[256,4,128]{2,1,0:T(4,128)} %param.7) | copy-start | bytes 1572868
  2.7 5.9 %copy-start.4 = (f32[256,4,128]{2,1,0:T(4,128)S(1)}, f32[256,4,128]{2,1,0:T(4,128)}, u32[]{:S(2)}) copy-start(f32[256,4,128]{2,1,0:T(4,128)} %param.8) | copy-start | bytes 1572868
  2.7 5.9 %copy-start.5 = (f32[256,4,128]{2,1,0:T(4,128)S(1)}, f32[256,4,128]{2,1,0:T(4,128)}, u32[]{:S(2)}) copy-start(f32[256,4,128]{2,1,0:T(4,128)} %param.11) | copy-start | bytes 1572868
  2.7 5.9 %copy-start.15 = (f32[4,128]{1,0:T(4,128)S(1)}, f32[4,128]{1,0:T(4,128)}, u32[]{:S(2)}) copy-start(f32[4,128]{1,0:T(4,128)} %key_gain_ref.5) | copy-start | bytes 6148
  3.0 5.7 %copy-start.14 = (f32[4,128]{1,0:T(4,128)S(1)}, f32[4,128]{1,0:T(4,128)}, u32[]{:S(2)}) copy-start(f32[4,128]{1,0:T(4,128)} %query_gain_ref.5) | copy-start | bytes 6148
  3.0 7.4 %collective-permute-start.2 = (f32[2,256]{1,0:T(2,128)S(1)}, f32[2,256]{1,0:T(2,128)S(1)}, u32[]{:S(2)}, u32[]{:S(2)}) collective-permute-start(f32[2,256]{1,0:T(2,128)S(1)} %squares.1.refs_0_), channel_id=1, source_target_pairs={{0,1},{1,0},{2,3},{3,2},{4,5},{5,4},{6,7},{7,6},{8,9},{9,8},{10,11... | collective-permute-start | bytes 6152 | tf_op jit(solution)/shard_map/ppermute | solution.py:237
  6.0 4.5 %collective-permute-start.1 = (f32[2,256]{1,0:T(2,128)S(1)}, f32[2,256]{1,0:T(2,128)S(1)}, u32[]{:S(2)}, u32[]{:S(2)}) collective-permute-start(f32[2,256]{1,0:T(2,128)S(1)} %squares.1.refs_0_), channel_id=1, source_target_pairs={{0,2},{1,3},{2,0},{3,1},{4,6},{5,7},{6,4},{7,5},{8,10},{9,11},{10,... | collective-permute-start | bytes 6152 | tf_op jit(solution)/shard_map/ppermute | solution.py:237
  8.6 5.4 %collective-permute-start = (f32[2,256]{1,0:T(2,128)S(1)}, f32[2,256]{1,0:T(2,128)S(1)}, u32[]{:S(2)}, u32[]{:S(2)}) collective-permute-start(f32[2,256]{1,0:T(2,128)S(1)} %squares.1.refs_0_), channel_id=1, source_target_pairs={{0,3},{1,2},{2,1},{3,0},{4,7},{5,6},{6,5},{7,4},{8,11},{9,10},{10,... | collective-permute-start | bytes 6152 | tf_op jit(solution)/shard_map/ppermute | solution.py:237
  9.5 0.8 %copy-start.6 = (bf16[4,256,256]{2,1,0:T(8,128)(2,1)}, bf16[4,256,256]{2,1,0:T(8,128)(2,1)S(1)}, u32[]{:S(2)}) copy-start(bf16[4,256,256]{2,1,0:T(8,128)(2,1)S(1)} %get-tuple-element.35.score_high_ref) | copy-start | bytes 1572868
  10.3 4.1 %copy-start.8 = (bf16[4,256,256]{2,1,0:T(8,128)(2,1)}, bf16[4,256,256]{2,1,0:T(8,128)(2,1)S(1)}, u32[]{:S(2)}) copy-start(bf16[4,256,256]{2,1,0:T(8,128)(2,1)S(1)} %get-tuple-element.36.score_low_ref) | copy-start | bytes 1572868
  10.3 4.2 %copy-start.10 = (bf16[4,256,256]{2,1,0:T(8,128)(2,1)}, bf16[4,256,256]{2,1,0:T(8,128)(2,1)S(1)}, u32[]{:S(2)}) copy-start(bf16[4,256,256]{2,1,0:T(8,128)(2,1)S(1)} %get-tuple-element.37.mix_high_ref) | copy-start | bytes 1572868
  10.3 4.2 %copy-start.12 = (bf16[4,256,256]{2,1,0:T(8,128)(2,1)}, bf16[4,256,256]{2,1,0:T(8,128)(2,1)S(1)}, u32[]{:S(2)}) copy-start(bf16[4,256,256]{2,1,0:T(8,128)(2,1)S(1)} %get-tuple-element.38.mix_low_ref) | copy-start | bytes 1572868
  14.5 1.6 %collective-permute-start.3 = (f32[512,128]{1,0:T(8,128)S(1)}, f32[512,128]{1,0:T(8,128)S(1)}, u32[]{:S(2)}, u32[]{:S(2)}) collective-permute-start(f32[512,128]{1,0:T(8,128)S(1)} %get-tuple-element.32), channel_id=1, source_target_pairs={{0,4},{4,0},{8,12},{12,8},{16,20},{20,16},{24,28},{28,24},{1,5},{5... | collective-permute-start | bytes 786440 | tf_op jit(solution)/shard_map/ppermute | solution.py:260
  14.6 1.9 %collective-permute-start.4 = (f32[512,128]{1,0:T(8,128)S(1)}, f32[512,128]{1,0:T(8,128)S(1)}, u32[]{:S(2)}, u32[]{:S(2)}) collective-permute-start(f32[512,128]{1,0:T(8,128)S(1)} %get-tuple-element.33), channel_id=1, source_target_pairs={{0,4},{4,0},{8,12},{12,8},{16,20},{20,16},{24,28},{28,24},{1,5},{5... | collective-permute-start | bytes 786440 | tf_op jit(solution)/shard_map/ppermute | solution.py:261
  16.1 1.1 %copy-start.16 = (f32[512,128]{1,0:T(8,128)}, f32[512,128]{1,0:T(8,128)S(1)}, u32[]{:S(2)}) copy-start(f32[512,128]{1,0:T(8,128)S(1)} %collective-permute-done.3) | copy-start | bytes 786436
  16.5 0.7 %copy-start.18 = (f32[512,128]{1,0:T(8,128)}, f32[512,128]{1,0:T(8,128)S(1)}, u32[]{:S(2)}) copy-start(f32[512,128]{1,0:T(8,128)S(1)} %collective-permute-done.4) | copy-start | bytes 786436
  17.2 5.7 %collective-permute-start.5 = (f32[256,128]{1,0:T(8,128)}, f32[256,128]{1,0:T(8,128)S(1)}, u32[]{:S(2)}, u32[]{:S(2)}) collective-permute-start(f32[256,128]{1,0:T(8,128)} %get-tuple-element.52), channel_id=1, source_target_pairs={{0,8},{4,12},{8,0},{12,4},{16,24},{20,28},{24,16},{28,20},{1,9},{5... | collective-permute-start | bytes 393224 | tf_op jit(solution)/shard_map/ppermute | solution.py:290
  19.4 8.3 %collective-permute-start.6 = (f32[256,128]{1,0:T(8,128)}, f32[256,128]{1,0:T(8,128)S(1)}, u32[]{:S(2)}, u32[]{:S(2)}) collective-permute-start(f32[256,128]{1,0:T(8,128)} %get-tuple-element.59), channel_id=1, source_target_pairs={{0,16},{4,20},{8,24},{12,28},{16,0},{20,4},{24,8},{28,12},{1,17},{... | collective-permute-start | bytes 393224 | tf_op jit(solution)/shard_map/ppermute | solution.py:290
  20.9 7.4 %collective-permute-start.7 = (f32[256,128]{1,0:T(8,128)}, f32[256,128]{1,0:T(8,128)}, u32[]{:S(2)}, u32[]{:S(2)}) collective-permute-start(f32[256,128]{1,0:T(8,128)} %get-tuple-element.60), channel_id=1, source_target_pairs={{0,24},{4,28},{8,16},{12,20},{16,8},{20,12},{24,0},{28,4},{1,25},{... | collective-permute-start | bytes 393224 | tf_op jit(solution)/shard_map/ppermute | solution.py:290
  21.4 8.7 %copy-start.1 = (f32[256,4,128]{2,1,0:T(4,128)S(1)}, f32[256,4,128]{2,1,0:T(4,128)}, u32[]{:S(2)}) copy-start(f32[256,4,128]{2,1,0:T(4,128)} %param.6) | copy-start | bytes 1572868
  21.4 8.7 %copy-start.3 = (f32[256,4,128]{2,1,0:T(4,128)S(1)}, f32[256,4,128]{2,1,0:T(4,128)}, u32[]{:S(2)}) copy-start(f32[256,4,128]{2,1,0:T(4,128)} %param.7) | copy-start | bytes 1572868
  27.7 0.6 %copy-start.20 = (f32[256,128]{1,0:T(8,128)}, f32[256,128]{1,0:T(8,128)S(1)}, u32[]{:S(2)}) copy-start(f32[256,128]{1,0:T(8,128)S(1)} %collective-permute-done.6) | copy-start | bytes 393220
  30.1 5.9 %collective-permute-start.8 = (f32[512,128]{1,0:T(8,128)}, f32[512,128]{1,0:T(8,128)}, u32[]{:S(2)}, u32[]{:S(2)}) collective-permute-start(f32[512,128]{1,0:T(8,128)} %pad_maximum_fusion.1), channel_id=1, source_target_pairs={{0,4},{4,0},{8,12},{12,8},{16,20},{20,16},{24,28},{28,24},{1,5},{5... | collective-permute-start | bytes 786440 | tf_op jit(solution)/shard_map/ppermute | solution.py:300
  30.1 1.0 %copy-start.7 = (bf16[4,256,256]{2,1,0:T(8,128)(2,1)S(1)}, bf16[4,256,256]{2,1,0:T(8,128)(2,1)}, u32[]{:S(2)}) copy-start(bf16[4,256,256]{2,1,0:T(8,128)(2,1)} %copy-done.6) | copy-start | bytes 1572868
  31.1 1.0 %copy-start.9 = (bf16[4,256,256]{2,1,0:T(8,128)(2,1)S(1)}, bf16[4,256,256]{2,1,0:T(8,128)(2,1)}, u32[]{:S(2)}) copy-start(bf16[4,256,256]{2,1,0:T(8,128)(2,1)} %copy-done.8) | copy-start | bytes 1572868
  32.2 1.0 %copy-start.11 = (bf16[4,256,256]{2,1,0:T(8,128)(2,1)S(1)}, bf16[4,256,256]{2,1,0:T(8,128)(2,1)}, u32[]{:S(2)}) copy-start(bf16[4,256,256]{2,1,0:T(8,128)(2,1)} %copy-done.10) | copy-start | bytes 1572868
  33.2 1.0 %copy-start.13 = (bf16[4,256,256]{2,1,0:T(8,128)(2,1)S(1)}, bf16[4,256,256]{2,1,0:T(8,128)(2,1)}, u32[]{:S(2)}) copy-start(bf16[4,256,256]{2,1,0:T(8,128)(2,1)} %copy-done.12) | copy-start | bytes 1572868
  36.0 1.1 %copy-start.17 = (f32[512,128]{1,0:T(8,128)S(1)}, f32[512,128]{1,0:T(8,128)}, u32[]{:S(2)}) copy-start(f32[512,128]{1,0:T(8,128)} %copy-done.16) | copy-start | bytes 786436
  36.0 1.1 %copy-start.19 = (f32[512,128]{1,0:T(8,128)S(1)}, f32[512,128]{1,0:T(8,128)}, u32[]{:S(2)}) copy-start(f32[512,128]{1,0:T(8,128)} %copy-done.18) | copy-start | bytes 786436
  38.8 4.9 %collective-permute-start.11 = (f32[2,256]{1,0:T(2,128)S(1)}, f32[2,256]{1,0:T(2,128)S(1)}, u32[]{:S(2)}, u32[]{:S(2)}) collective-permute-start(f32[2,256]{1,0:T(2,128)S(1)} %get-tuple-element.44.refs_0_), channel_id=1, source_target_pairs={{0,1},{1,0},{2,3},{3,2},{4,5},{5,4},{6,7},{7,6},{8,9},{9,8},{10,11... | collective-permute-start | bytes 6152 | tf_op jit(solution)/shard_map/ppermute | solution.py:237
  38.8 4.9 %collective-permute-start.10 = (f32[2,256]{1,0:T(2,128)S(1)}, f32[2,256]{1,0:T(2,128)S(1)}, u32[]{:S(2)}, u32[]{:S(2)}) collective-permute-start(f32[2,256]{1,0:T(2,128)S(1)} %get-tuple-element.44.refs_0_), channel_id=1, source_target_pairs={{0,2},{1,3},{2,0},{3,1},{4,6},{5,7},{6,4},{7,5},{8,10},{9,11},{10,... | collective-permute-start | bytes 6152 | tf_op jit(solution)/shard_map/ppermute | solution.py:237
  40.1 5.4 %collective-permute-start.9 = (f32[2,256]{1,0:T(2,128)S(1)}, f32[2,256]{1,0:T(2,128)S(1)}, u32[]{:S(2)}, u32[]{:S(2)}) collective-permute-start(f32[2,256]{1,0:T(2,128)S(1)} %get-tuple-element.44.refs_0_), channel_id=1, source_target_pairs={{0,3},{1,2},{2,1},{3,0},{4,7},{5,6},{6,5},{7,4},{8,11},{9,10},{10,... | collective-permute-start | bytes 6152 | tf_op jit(solution)/shard_map/ppermute | solution.py:237
